TPU v7x, 32 devices: a whole 2x2x4 slice. The times are simulated.
32 devices in a mesh: win: 2 (over y), row: 16 (over z, x, core).
Axes of the slice: x: 2, y: 2, z: 4, core: 2. Of those that a mesh axis runs over, the one named last changes fastest.
Arguments:
- spectra: bfloat16 [32, 2, 32768], P(('win', 'row')), parts along dimension 0, may hold values from -6 to 6
- pair_mask: int32 [16, 16], P('row'), may hold values from 0 to 1, as said below
- available: int32 [32], P('win'), parts along dimension 0, may hold values 0 or 1
Outputs:
- correlations: float32 [32, 16, 8192], P(('win', 'row')), parts along dimension 0
There are 2 independent parts, one for each index of `win`. A program takes and returns all parts, laid end to end along the dimension named above; an argument that names none is the same for every part. Nothing has to cross between parts.
Inputs may be any that keep to these rules, and one draw needn't show every extreme that they name: pair_mask[i, j] is 0 wherever j <= i.
All inputs are finite; a program needn't handle non-finite values.
Results may differ from a plain program's by a relative error of at most 0.0003.
Values may be sent and summed in bfloat16 or wider, within the bound.
A program may use at most 128 MiB of HBM per device.

v0:
```python
import math
import jax
import jax.numpy as jnp
from jax import lax
from jax.sharding import PartitionSpec as P

LAGS = 8192
full_turn = 2.0 * math.pi


def shifted(value, axis, by):
    size = lax.axis_size(axis)
    return lax.ppermute(value, axis, [(i, (i + by) % size) for i in range(size)])


def build_tables(freq, lags):
    nfft = 2 * freq
    inner = min(128, lags // 2)
    column = nfft // inner
    depth = freq // column
    outer = lags // inner
    centre = lags // 2
    t_inner = jnp.arange(inner, dtype=jnp.int32)
    k_depth = jnp.arange(depth, dtype=jnp.int32)
    k_column = jnp.arange(column, dtype=jnp.int32)
    t_outer = jnp.arange(outer, dtype=jnp.int32)
    first = full_turn * (t_inner[:, None] * k_depth[None, :] % inner).astype(jnp.float32) / inner
    cos_first = jnp.cos(first)
    sin_first = jnp.sin(first)
    section_one = jnp.concatenate(
        [
            jnp.concatenate([cos_first, -sin_first], axis=1),
            jnp.concatenate([sin_first, cos_first], axis=1),
        ],
        axis=0,
    )
    twist = (
        full_turn
        * jnp.mod(k_column[None, :] * (t_inner[:, None] - centre), nfft).astype(jnp.float32)
        / nfft
    )
    second = (
        full_turn * (t_outer[:, None] * k_column[None, :] % column).astype(jnp.float32) / column
    )
    section_two = jnp.stack([jnp.cos(second), -jnp.sin(second)], axis=1)
    return (section_one, jnp.cos(twist), jnp.sin(twist), section_two)


def pair_block(own_wide, part, signs, tables):
    section_one, twist_cos, twist_sin, section_two = tables
    count = own_wide.shape[0]
    width = part.shape[0]
    freq = part.shape[2]
    inner = twist_cos.shape[0]
    column = twist_cos.shape[1]
    outer = section_two.shape[0]
    depth = freq // column
    other = part.astype(jnp.float32)
    real_part = (
        own_wide[:, None, 0, :] * other[None, :, 0, :]
        + own_wide[:, None, 1, :] * other[None, :, 1, :]
    )
    imag_part = (
        own_wide[:, None, 0, :] * other[None, :, 1, :]
        - own_wide[:, None, 1, :] * other[None, :, 0, :]
    ) * signs[:, :, None]
    cross = jnp.stack([real_part, imag_part], axis=2).reshape(count * width, 2 * depth, column)
    mixed = jnp.einsum("uv,pvk->puk", section_one, cross, precision=lax.Precision.HIGH)
    mixed = mixed.reshape(count * width, 2, inner, column)
    turned_real = mixed[:, 0] * twist_cos - mixed[:, 1] * twist_sin
    turned_imag = mixed[:, 0] * twist_sin + mixed[:, 1] * twist_cos
    turned = jnp.stack([turned_real, turned_imag], axis=1)
    summed = jnp.einsum("tck,pcuk->ptu", section_two, turned, precision=lax.Precision.HIGH)
    summed = summed.reshape(count, width, outer * inner)
    return (2.0 * summed - real_part[:, :, :1]) * (1.0 / math.sqrt(8.0 * freq))


def correlate(own, others, signs, tables):
    own_wide = own.astype(jnp.float32)
    count = own.shape[0]
    total = others.shape[0]
    width = math.gcd(total, max(1, 8 // count))
    if width == total:
        return pair_block(own_wide, others, signs, tables)
    groups = total // width
    pieces = others.reshape(groups, width, 2, others.shape[2])
    sign_pieces = jnp.transpose(signs.reshape(count, groups, width), (1, 0, 2))

    def one_group(item):
        return pair_block(own_wide, item[0], item[1], tables)

    results = lax.map(one_group, (pieces, sign_pieces))
    return jnp.transpose(results, (1, 0, 2, 3)).reshape(count, total, results.shape[3])


def per_device(spectra, pair_mask, available):
    count = spectra.shape[0]
    devices = lax.axis_size("row")
    stations = count * devices
    freq = spectra.shape[2]
    tables = build_tables(freq, LAGS)
    first_station = lax.axis_index("row") * count
    own_flags = lax.dynamic_slice_in_dim(available, first_station, count, 0).astype(jnp.float32)
    weight = (
        pair_mask.astype(jnp.float32) * own_flags[:, None] * available.astype(jnp.float32)[None, :]
    )
    reach = devices // 2 + 1
    window = spectra
    have = 1
    while have < reach:
        take = min(have, reach - have)
        moved = shifted(window[: take * count], "row", -have)
        window = jnp.concatenate([window, moved], axis=0)
        have = have + take
    half = stations // 2
    offsets = jnp.arange(half, dtype=jnp.int32) + 1
    columns = jnp.arange(stations, dtype=jnp.int32)
    station = first_station + 0
    signs = jnp.where(station + offsets >= stations, -1.0, 1.0).astype(jnp.float32)[None, :]
    near = correlate(window[0:1], window[1 : 1 + half], signs, tables)[0]
    padded = jnp.concatenate([near, jnp.zeros_like(near)], axis=0)
    placed = jnp.roll(padded, station + 1, axis=0)
    keep_rows = [jnp.where((columns > station)[:, None], placed, 0.0)]
    send_rows = [jnp.where((columns < station - half)[:, None], placed, 0.0)]
    kept = jnp.stack(keep_rows, axis=0)
    outgoing = jnp.stack(send_rows, axis=1)
    incoming = lax.all_to_all(outgoing, "row", split_axis=0, concat_axis=1, tiled=True)
    corr = kept + incoming
    return corr * weight[:, :, None]


def solution(mesh):
    return jax.shard_map(
        per_device,
        mesh=mesh,
        in_specs=(P(("win", "row"), None, None), P("row", None), P("win")),
        out_specs=P(("win", "row"), None, None),
        check_vma=False,
    )
```

profile of v0, /device:TPU:0, one launch (start us, length us, event | category | flops | bytes accessed | tf_op | source)
XLA Modules:
  0.0 77.3 jit_solution(7756633121859793812)
XLA Ops:
  0.0 5.4 %collective-permute-start = (bf16[1,2,32768]{2,1,0:T(2,128)(2,1)}, bf16[1,2,32768]{2,1,0:T(2,128)(2,1)S(1)}, u32[]{:S(2)}, u32[]{:S(2)}) collective-permute-start(bf16[1,2,32768]{2,1,0:T(2,128)(2,1)} %param.3), channel_id=1, source_target_pairs={{0,15},{1,0},{2,1},{3,2},{4,3},{5,4},{6,5},{7,6},{8,7},{9,8},{10,9... | collective-permute-start | bytes 393224 | tf_op jit(solution)/shard_map/ppermute | solution.py:13
  5.4 1.2 %fusion.60 = (f32[1,1,32768]{2,1,0:T(1,128)S(1)}, f32[1,1,32768]{2,1,0:T(1,128)S(1)}) fusion(bf16[1,2,32768]{2,1,0:T(2,128)(2,1)} %param.3), kind=kLoop, calls=%fused_computation.92 | loop fusion | bytes 524288 | tf_op jit(solution)/shard_map/slice | solution.py:60
  6.7 1.6 %collective-permute-done = bf16[1,2,32768]{2,1,0:T(2,128)(2,1)S(1)} collective-permute-done((bf16[1,2,32768]{2,1,0:T(2,128)(2,1)}, bf16[1,2,32768]{2,1,0:T(2,128)(2,1)S(1)}, u32[]{:S(2)}, u32[]{:S(2)}) %collective-permute-start) | collective-permute-done | bytes 131104 | tf_op jit(solution)/shard_map/ppermute | solution.py:13
  8.3 1.3 %pad_maximum_fusion.2 = bf16[2,2,32768]{2,1,0:T(2,128)(2,1)S(1)} fusion(bf16[1,2,32768]{2,1,0:T(2,128)(2,1)S(1)} %collective-permute-done, bf16[1,2,32768]{2,1,0:T(2,128)(2,1)} %param.3), kind=kLoop, calls=%fused_computation.37 | loop fusion | flops 131072 | bytes 524288 | tf_op jit(solution)/shard_map/concatenate | solution.py:113
  10.2 0.9 %fusion.54 = f32[128,64]{1,0:T(8,128)} fusion(), kind=kLoop, calls=%fused_computation.79 | loop fusion | flops 122880 | bytes 32768 | tf_op jit(solution)/shard_map/neg | solution.py:32
  11.1 0.9 %fusion.52 = (f32[128,64]{1,0:T(8,128)}, f32[128,64]{1,0:T(8,128)}) fusion(), kind=kLoop, calls=%fused_computation.77 | loop fusion | flops 114688 | bytes 65536 | tf_op jit(solution)/shard_map/sin | solution.py:29
  12.0 5.5 %collective-permute-done.1 = bf16[2,2,32768]{2,1,0:T(2,128)(2,1)S(1)} collective-permute-done((bf16[2,2,32768]{2,1,0:T(2,128)(2,1)S(1)}, bf16[2,2,32768]{2,1,0:T(2,128)(2,1)S(1)}, u32[]{:S(2)}, u32[]{:S(2)}) %collective-permute-start.1) | collective-permute-done | bytes 262176 | tf_op jit(solution)/shard_map/ppermute | solution.py:13
  17.5 1.7 %pad_maximum_fusion.1 = bf16[4,2,32768]{2,1,0:T(2,128)(2,1)S(1)} fusion(bf16[2,2,32768]{2,1,0:T(2,128)(2,1)S(1)} %collective-permute-done.1, bf16[1,2,32768]{2,1,0:T(2,128)(2,1)S(1)} %collective-permute-done, bf16[1,2,32768]{2,1,0:T(2,128)(2,1)} %param.3), kind=kLoop, calls=%fused_computation.25 | loop fusion | flops 524288 | bytes 1048576 | tf_op jit(solution)/shard_map/concatenate | solution.py:113
  19.6 1.9 %fusion.43 = (f32[128,512]{1,0:T(8,128)S(1)}, f32[128,512]{1,0:T(8,128)}) fusion(s32[128]{0:T(128)S(1)} %iota_add_fusion), kind=kLoop, calls=%fused_computation.63 | loop fusion | flops 917504 | bytes 524800 | tf_op jit(solution)/shard_map/cos | solution.py:46
  22.6 1.2 %sine_negate_fusion = (f32[64,1,512]{2,0,1:T(8,128)S(1)}, f32[64,1,512]{2,0,1:T(8,128)}) fusion(), kind=kLoop, calls=%fused_computation.59 | loop fusion | flops 491520 | bytes 262144 | tf_op jit(solution)/shard_map/neg | solution.py:45
  23.8 9.3 %collective-permute-done.2 = bf16[4,2,32768]{2,1,0:T(2,128)(2,1)S(1)} collective-permute-done((bf16[4,2,32768]{2,1,0:T(2,128)(2,1)S(1)}, bf16[4,2,32768]{2,1,0:T(2,128)(2,1)S(1)}, u32[]{:S(2)}, u32[]{:S(2)}) %collective-permute-start.2) | collective-permute-done | bytes 524320 | tf_op jit(solution)/shard_map/ppermute | solution.py:13
  33.1 1.4 %maximum_convert_fusion = f32[8,2,32768]{2,1,0:T(2,128)S(1)} fusion(bf16[1,2,32768]{2,1,0:T(2,128)(2,1)S(1)} %collective-permute-done.3, bf16[4,2,32768]{2,1,0:T(2,128)(2,1)S(1)} %collective-permute-done.2, bf16[2,2,32768]{2,1,0:T(2,128)(2,1)S(1)} %collective-permute-done.1, bf16[1,2,32768]{2,1,0:T(2,128)(2,1)S(1)} %collective-permute-done), kind=kLoop, calls=%fused_computation.10 | loop fusion | flops 2097152 | bytes 3145728 | tf_op jit(solution)/shard_map/convert_element_type | solution.py:58
  34.5 3.0 %slice_bitcast_fusion.1 = (f32[1,8,32768]{2,0,1:T(1,128)S(1)}, f32[1,8,32768]{2,0,1:T(1,128)}) fusion(f32[8,2,32768]{2,1,0:T(2,128)S(1)} %maximum_convert_fusion), kind=kLoop, calls=%fused_computation.76 | loop fusion | bytes 4194304 | tf_op jit(solution)/shard_map/broadcast_in_dim;squeeze | solution.py:60
  37.5 2.6 %fusion.13 = (f32[1,8,1,32768]{3,2,1,0:T(1,128)S(1)}, f32[1,8,1,32768]{3,2,1,0:T(1,128)S(1)}) fusion(f32[32768]{0:T(1024)S(1)} %bitcast.65, f32[32768]{0:T(1024)S(1)} %bitcast.63, f32[8,2,32768]{2,1,0:T(2,128)S(1)} %maximum_convert_fusion, f32[8]{0:T(128)S(1)} %compare_select_fusion), kind=kLoop, calls=%fused_computation.17 | loop fusion | flops 1835008 | bytes 4456480 | tf_op jit(solution)/shard_map/add | solution.py:60
  40.1 3.2 %pad_maximum_fusion = f32[1,8,2,32768]{3,2,1,0:T(2,128)} fusion(f32[1,8,1,32768]{3,2,1,0:T(1,128)S(1)} %get-tuple-element.8, f32[1,8,1,32768]{3,2,1,0:T(1,128)S(1)} %get-tuple-element.7), kind=kLoop, calls=%fused_computation.4 | loop fusion | flops 524288 | bytes 4194304 | tf_op jit(solution)/shard_map/stack | solution.py:67
  43.3 3.2 %reshape.460 = f32[8,128,512]{2,1,0:T(8,128)S(1)} reshape(f32[1,8,2,32768]{3,2,1,0:T(2,128)} %pad_maximum_fusion) | data formatting | bytes 4194304 | tf_op jit(solution)/shard_map/reshape | solution.py:67
  46.6 3.2 %fusion.33 = f32[8,512,256]{1,2,0:T(8,128)S(1)} fusion(f32[8,128,512]{2,1,0:T(8,128)S(1)} %reshape.460, f32[128,64]{1,0:T(8,128)} %get-tuple-element.16, f32[128,64]{1,0:T(8,128)} %get-tuple-element.15, f32[128,64]{1,0:T(8,128)} %fusion.54), kind=kOutput, calls=%fused_computation.52 | convolution fusion | flops 805404672 | bytes 6389760 | tf_op jit(solution)/shard_map/uv,pvk->puk/dot_general | solution.py:68
  49.8 0.7 multiply_subtract_fusion
  50.5 2.1 %fusion.56 = f32[8]{0:T(128)S(1)} fusion(f32[1,8,32768]{2,0,1:T(1,128)} %get-tuple-element.10, f32[1,8,32768]{2,0,1:T(1,128)S(1)} %get-tuple-element.9, f32[1]{0:T(128)} %slice.44, f32[1]{0:T(128)} %slice.42), kind=kLoop, calls=%fused_computation.83 | loop fusion | flops 24 | bytes 104 | tf_op jit(solution)/shard_map/slice | solution.py:75
  52.5 2.0 %fusion.10 = f32[1,8,64,128]{3,2,1,0:T(8,128)S(1)} fusion(f32[8,1,128,512]{3,2,1,0:T(8,128)S(1)} %get-tuple-element.6, f32[8,1,128,512]{3,2,1,0:T(8,128)S(1)} %get-tuple-element.5, f32[64,1,512]{2,0,1:T(8,128)S(1)} %get-tuple-element.17, f32[64,1,512]{2,0,1:T(8,128)S(1)} %copy-done.1), kind=kOutput, calls=%fused_computation.9 | convolution fusion | flops 403832832 | bytes 4718592 | tf_op jit(solution)/shard_map/tck,pcuk->ptu/dot_general | solution.py:73
  55.1 1.3 %stack.22 = f32[16,1,8192]{2,1,0:T(1,128)} reshape(f32[16,8192]{1,0:T(8,128)S(1)} %broadcast_select_fusion) | data formatting | bytes 1048576 | tf_op jit(solution)/shard_map/stack | solution.py:126
  56.4 5.4 %all-to-all-start = ((f32[16,1,8192]{2,1,0:T(1,128)}), f32[16,1,8192]{2,1,0:T(1,128)S(1)}, u32[]{:S(2)}, u32[]{:S(2)}) async-start(f32[16,1,8192]{2,1,0:T(1,128)} %stack.22), calls=%async_computation | async-start | bytes 1048576 | tf_op jit(solution)/shard_map/all_to_all | solution.py:127
  63.1 13.0 %all-to-all-done = f32[16,1,8192]{2,1,0:T(1,128)S(1)} async-done(((f32[16,1,8192]{2,1,0:T(1,128)}), f32[16,1,8192]{2,1,0:T(1,128)S(1)}, u32[]{:S(2)}, u32[]{:S(2)}) %all-to-all-start) | async-done | bytes 524320 | tf_op jit(solution)/shard_map/all_to_all | solution.py:127
  76.1 1.2 %fusion.20 = f32[1,16,8192]{2,1,0:T(8,128)} fusion(f32[16,1,8192]{2,1,0:T(1,128)S(1)} %all-to-all-done, f32[16]{0:T(128)S(1)} %fusion.57, pred[16]{0:T(512)(128)(4,1)S(1)} %iota_compare_fusion.1, s32[]{:T(128)S(6)} %select_n.86, f32[8,8192]{1,0:T(8,128)S(1)} %broadcast_in_dim.49, f32[8,8192]{1,0:T(8,128)S(1)} %fusion.24), kind=kLoop, calls=%fused_computation.28 | loop fusion | flops 786432 | bytes 1572948 | tf_op jit(solution)/shard_map/mul | solution.py:129
  (23 shorter events, 3.2 us)
Async XLA Ops:
  0.0 8.3 %collective-permute-start = (bf16[1,2,32768]{2,1,0:T(2,128)(2,1)}, bf16[1,2,32768]{2,1,0:T(2,128)(2,1)S(1)}, u32[]{:S(2)}, u32[]{:S(2)}) collective-permute-start(bf16[1,2,32768]{2,1,0:T(2,128)(2,1)} %param.3), channel_id=1, source_target_pairs={{0,15},{1,0},{2,1},{3,2},{4,3},{5,4},{6,5},{7,6},{8,7},{9,8},{10,9... | collective-permute-start | bytes 393224 | tf_op jit(solution)/shard_map/ppermute | solution.py:13
  5.4 18.3 %collective-permute-start.3 = (bf16[1,2,32768]{2,1,0:T(2,128)(2,1)}, bf16[1,2,32768]{2,1,0:T(2,128)(2,1)S(1)}, u32[]{:S(2)}, u32[]{:S(2)}) collective-permute-start(bf16[1,2,32768]{2,1,0:T(2,128)(2,1)} %param.3), channel_id=1, source_target_pairs={{0,8},{1,9},{2,10},{3,11},{4,12},{5,13},{6,14},{7,15},{8,0},{9,1},... | collective-permute-start | bytes 393224 | tf_op jit(solution)/shard_map/ppermute | solution.py:13
  9.6 8.0 %collective-permute-start.1 = (bf16[2,2,32768]{2,1,0:T(2,128)(2,1)S(1)}, bf16[2,2,32768]{2,1,0:T(2,128)(2,1)S(1)}, u32[]{:S(2)}, u32[]{:S(2)}) collective-permute-start(bf16[2,2,32768]{2,1,0:T(2,128)(2,1)S(1)} %pad_maximum_fusion.2), channel_id=1, source_target_pairs={{0,14},{1,15},{2,0},{3,1},{4,2},{5,3},{6,4},{7,5},{8,6},{9,7},{10,... | collective-permute-start | bytes 786440 | tf_op jit(solution)/shard_map/ppermute | solution.py:13
  19.2 13.9 %collective-permute-start.2 = (bf16[4,2,32768]{2,1,0:T(2,128)(2,1)S(1)}, bf16[4,2,32768]{2,1,0:T(2,128)(2,1)S(1)}, u32[]{:S(2)}, u32[]{:S(2)}) collective-permute-start(bf16[4,2,32768]{2,1,0:T(2,128)(2,1)S(1)} %pad_maximum_fusion.1), channel_id=1, source_target_pairs={{0,12},{1,13},{2,14},{3,15},{4,0},{5,1},{6,2},{7,3},{8,4},{9,5},{1... | collective-permute-start | bytes 1572872 | tf_op jit(solution)/shard_map/ppermute | solution.py:13
  46.5 3.2 %copy-start = (f32[128,512]{1,0:T(8,128)S(1)}, f32[128,512]{1,0:T(8,128)}, u32[]{:S(2)}) copy-start(f32[128,512]{1,0:T(8,128)} %get-tuple-element.14) | copy-start | bytes 786436
  49.8 2.8 %copy-start.1 = (f32[64,1,512]{2,0,1:T(8,128)S(1)}, f32[64,1,512]{2,0,1:T(8,128)}, u32[]{:S(2)}) copy-start(f32[64,1,512]{2,0,1:T(8,128)} %get-tuple-element.18) | copy-start | bytes 393220
  54.6 7.3 %copy-start.2 = (s32[16]{0:T(128)S(1)}, s32[16]{0:T(128)}, u32[]{:S(2)}) copy-start(s32[16]{0:T(128)} %param.5) | copy-start | bytes 196
  54.6 8.5 %copy-start.3 = (s32[1,16]{1,0:T(1,128)S(1)}, s32[1,16]{1,0:T(1,128)}, u32[]{:S(2)}) copy-start(s32[1,16]{1,0:T(1,128)} %param.4) | copy-start | bytes 196
  56.4 19.7 %all-to-all-start = ((f32[16,1,8192]{2,1,0:T(1,128)}), f32[16,1,8192]{2,1,0:T(1,128)S(1)}, u32[]{:S(2)}, u32[]{:S(2)}) async-start(f32[16,1,8192]{2,1,0:T(1,128)} %stack.22), calls=%async_computation | async-start | bytes 1048576 | tf_op jit(solution)/shard_map/all_to_all | solution.py:127
where the time goes:
time: 77.7 us; the launch traced here: 77.3 us
  waiting for transfers between devices  29.4 us (38%)
  other arithmetic  19.5 us (25%)
  starting transfers between devices  11.9 us (15%)
  local copies, waits for them, and re-layouts  10.5 us (14%)
  matrix products  5.22 us (7%)
  between operations  0.79 us (1%)
    ppermute x4, waiting for transfers between devices, shifted(): lax.ppermute(value, axis, [(i, (i + by) % size) for i in range(size)])  16.4 us
    all_to_all x1, waiting for transfers between devices, per_device(): lax.all_to_all(outgoing, 'row', split_axis=0, concat_axis=1, tiled=True)  13 us
    ppermute x4, starting transfers between devices, shifted(): lax.ppermute(value, axis, [(i, (i + by) % size) for i in range(size)])  6.45 us
    all_to_all x1, starting transfers between devices, per_device(): lax.all_to_all(outgoing, 'row', split_axis=0, concat_axis=1, tiled=True)  5.41 us
    reshape x1, local copies, waits for them, and re-layouts, pair_block(): jnp.stack([real_part, imag_part], axis=2)  3.23 us
    another operation x1, other arithmetic, pair_block(): jnp.stack([real_part, imag_part], axis=2)  3.2 us
    dot_general x1, matrix products, pair_block(): jnp.einsum('uv,pvk->puk', section_one, cross, precision=lax.Precision.HIGH)  3.19 us
    another operation x1, local copies, waits for them, and re-layouts, pair_block(): other[None, :, 0, :]  2.99 us
  transfers between devices with their start and end apart: 5, of which 4 were waited for; matrix products, arithmetic and copies ran while one was open for 14% of the time, Pallas kernels for 0%

commit v1 on v0

--- a/solution.py
+++ b/solution.py
@@ -124,7 +124,10 @@
     send_rows = [jnp.where((columns < station - half)[:, None], placed, 0.0)]
     kept = jnp.stack(keep_rows, axis=0)
     outgoing = jnp.stack(send_rows, axis=1)
-    incoming = lax.all_to_all(outgoing, "row", split_axis=0, concat_axis=1, tiled=True)
+    incoming = jnp.concatenate(
+        lax.all_to_all(jnp.stack(jnp.split(outgoing, lax.axis_size("row"), axis=0)), "row", 0, 0),
+        axis=1,
+    )
     corr = kept + incoming
     return corr * weight[:, :, None]
 

time: 77.7 us -> 86.7 us (1.12)
  local copies, waits for them, and re-layouts: 10.5 us -> 19.5 us
    unnamed x8 -> x23, local copies, waits for them, and re-layouts: 0.02 us -> 9.65 us
  transfers between devices with their start and end apart: 5 -> 5, of which waited for: 4 -> 4; matrix products, arithmetic and copies ran while one was open for 14% -> 13% of each run, Pallas kernels for 0% -> 0%
where the time goes in v1:
time: 86.7 us; the launch traced here: 86.3 us
  waiting for transfers between devices  29.4 us (34%)
  local copies, waits for them, and re-layouts  19.5 us (22%)
  other arithmetic  19.5 us (22%)
  starting transfers between devices  11.9 us (14%)
  matrix products  5.22 us (6%)
    ppermute x4, waiting for transfers between devices, shifted(): lax.ppermute(value, axis, [(i, (i + by) % size) for i in range(size)])  16.4 us
    all_to_all x1, waiting for transfers between devices, per_device(): lax.all_to_all(jnp.stack(jnp.split(outgoing, lax.axis_size('row'), axis=0...  13 us
    unnamed x23, local copies, waits for them, and re-layouts  9.65 us
    ppermute x4, starting transfers between devices, shifted(): lax.ppermute(value, axis, [(i, (i + by) % size) for i in range(size)])  6.45 us
    all_to_all x1, starting transfers between devices, per_device(): lax.all_to_all(jnp.stack(jnp.split(outgoing, lax.axis_size('row'), axis=0...  5.41 us
    reshape x1, local copies, waits for them, and re-layouts, pair_block(): jnp.stack([real_part, imag_part], axis=2)  3.23 us
    another operation x1, other arithmetic, pair_block(): jnp.stack([real_part, imag_part], axis=2)  3.2 us
    dot_general x1, matrix products, pair_block(): jnp.einsum('uv,pvk->puk', section_one, cross, precision=lax.Precision.HIGH)  3.19 us
  transfers between devices with their start and end apart: 5, of which 4 were waited for; matrix products, arithmetic and copies ran while one was open for 13% of the time, Pallas kernels for 0%

profile of v1, /device:TPU:0, one launch (start us, length us, event | category | flops | bytes accessed | tf_op | source)
XLA Modules:
  0.0 86.3 jit_solution(9119382263005383643)
XLA Ops:
  0.0 5.4 %collective-permute-start = (bf16[1,2,32768]{2,1,0:T(2,128)(2,1)}, bf16[1,2,32768]{2,1,0:T(2,128)(2,1)S(1)}, u32[]{:S(2)}, u32[]{:S(2)}) collective-permute-start(bf16[1,2,32768]{2,1,0:T(2,128)(2,1)} %param.3), channel_id=1, source_target_pairs={{0,15},{1,0},{2,1},{3,2},{4,3},{5,4},{6,5},{7,6},{8,7},{9,8},{10,9... | collective-permute-start | bytes 393224 | tf_op jit(solution)/shard_map/ppermute | solution.py:13
  5.4 1.2 %fusion.60 = (f32[1,1,32768]{2,1,0:T(1,128)S(1)}, f32[1,1,32768]{2,1,0:T(1,128)S(1)}) fusion(bf16[1,2,32768]{2,1,0:T(2,128)(2,1)} %param.3), kind=kLoop, calls=%fused_computation.124 | loop fusion | bytes 524288 | tf_op jit(solution)/shard_map/slice | solution.py:60
  6.7 1.6 %collective-permute-done = bf16[1,2,32768]{2,1,0:T(2,128)(2,1)S(1)} collective-permute-done((bf16[1,2,32768]{2,1,0:T(2,128)(2,1)}, bf16[1,2,32768]{2,1,0:T(2,128)(2,1)S(1)}, u32[]{:S(2)}, u32[]{:S(2)}) %collective-permute-start) | collective-permute-done | bytes 131104 | tf_op jit(solution)/shard_map/ppermute | solution.py:13
  8.3 1.3 %pad_maximum_fusion.2 = bf16[2,2,32768]{2,1,0:T(2,128)(2,1)S(1)} fusion(bf16[1,2,32768]{2,1,0:T(2,128)(2,1)S(1)} %collective-permute-done, bf16[1,2,32768]{2,1,0:T(2,128)(2,1)} %param.3), kind=kLoop, calls=%fused_computation.37 | loop fusion | flops 131072 | bytes 524288 | tf_op jit(solution)/shard_map/concatenate | solution.py:113
  10.2 0.9 %fusion.54 = f32[128,64]{1,0:T(8,128)} fusion(), kind=kLoop, calls=%fused_computation.111 | loop fusion | flops 122880 | bytes 32768 | tf_op jit(solution)/shard_map/neg | solution.py:32
  11.1 0.9 %fusion.52 = (f32[128,64]{1,0:T(8,128)}, f32[128,64]{1,0:T(8,128)}) fusion(), kind=kLoop, calls=%fused_computation.109 | loop fusion | flops 114688 | bytes 65536 | tf_op jit(solution)/shard_map/sin | solution.py:29
  12.0 5.5 %collective-permute-done.1 = bf16[2,2,32768]{2,1,0:T(2,128)(2,1)S(1)} collective-permute-done((bf16[2,2,32768]{2,1,0:T(2,128)(2,1)S(1)}, bf16[2,2,32768]{2,1,0:T(2,128)(2,1)S(1)}, u32[]{:S(2)}, u32[]{:S(2)}) %collective-permute-start.1) | collective-permute-done | bytes 262176 | tf_op jit(solution)/shard_map/ppermute | solution.py:13
  17.5 1.7 %pad_maximum_fusion.1 = bf16[4,2,32768]{2,1,0:T(2,128)(2,1)S(1)} fusion(bf16[2,2,32768]{2,1,0:T(2,128)(2,1)S(1)} %collective-permute-done.1, bf16[1,2,32768]{2,1,0:T(2,128)(2,1)S(1)} %collective-permute-done, bf16[1,2,32768]{2,1,0:T(2,128)(2,1)} %param.3), kind=kLoop, calls=%fused_computation.25 | loop fusion | flops 524288 | bytes 1048576 | tf_op jit(solution)/shard_map/concatenate | solution.py:113
  19.6 1.9 %fusion.43 = (f32[128,512]{1,0:T(8,128)S(1)}, f32[128,512]{1,0:T(8,128)}) fusion(s32[128]{0:T(128)S(1)} %iota_add_fusion), kind=kLoop, calls=%fused_computation.63 | loop fusion | flops 917504 | bytes 524800 | tf_op jit(solution)/shard_map/cos | solution.py:46
  22.6 1.2 %sine_negate_fusion = (f32[64,1,512]{2,0,1:T(8,128)S(1)}, f32[64,1,512]{2,0,1:T(8,128)}) fusion(), kind=kLoop, calls=%fused_computation.59 | loop fusion | flops 491520 | bytes 262144 | tf_op jit(solution)/shard_map/neg | solution.py:45
  23.8 9.3 %collective-permute-done.2 = bf16[4,2,32768]{2,1,0:T(2,128)(2,1)S(1)} collective-permute-done((bf16[4,2,32768]{2,1,0:T(2,128)(2,1)S(1)}, bf16[4,2,32768]{2,1,0:T(2,128)(2,1)S(1)}, u32[]{:S(2)}, u32[]{:S(2)}) %collective-permute-start.2) | collective-permute-done | bytes 524320 | tf_op jit(solution)/shard_map/ppermute | solution.py:13
  33.1 1.4 %maximum_convert_fusion = f32[8,2,32768]{2,1,0:T(2,128)S(1)} fusion(bf16[1,2,32768]{2,1,0:T(2,128)(2,1)S(1)} %collective-permute-done.3, bf16[4,2,32768]{2,1,0:T(2,128)(2,1)S(1)} %collective-permute-done.2, bf16[2,2,32768]{2,1,0:T(2,128)(2,1)S(1)} %collective-permute-done.1, bf16[1,2,32768]{2,1,0:T(2,128)(2,1)S(1)} %collective-permute-done), kind=kLoop, calls=%fused_computation.10 | loop fusion | flops 2097152 | bytes 3145728 | tf_op jit(solution)/shard_map/convert_element_type | solution.py:58
  34.5 3.0 %slice_bitcast_fusion.1 = (f32[1,8,32768]{2,0,1:T(1,128)S(1)}, f32[1,8,32768]{2,0,1:T(1,128)}) fusion(f32[8,2,32768]{2,1,0:T(2,128)S(1)} %maximum_convert_fusion), kind=kLoop, calls=%fused_computation.76 | loop fusion | bytes 4194304 | tf_op jit(solution)/shard_map/broadcast_in_dim;squeeze | solution.py:60
  37.5 2.6 %fusion.13 = (f32[1,8,1,32768]{3,2,1,0:T(1,128)S(1)}, f32[1,8,1,32768]{3,2,1,0:T(1,128)S(1)}) fusion(f32[32768]{0:T(1024)S(1)} %bitcast.129, f32[32768]{0:T(1024)S(1)} %bitcast.127, f32[8,2,32768]{2,1,0:T(2,128)S(1)} %maximum_convert_fusion, f32[8]{0:T(128)S(1)} %compare_select_fusion), kind=kLoop, calls=%fused_computation.17 | loop fusion | flops 1835008 | bytes 4456480 | tf_op jit(solution)/shard_map/add | solution.py:60
  40.1 3.2 %pad_maximum_fusion = f32[1,8,2,32768]{3,2,1,0:T(2,128)} fusion(f32[1,8,1,32768]{3,2,1,0:T(1,128)S(1)} %get-tuple-element.8, f32[1,8,1,32768]{3,2,1,0:T(1,128)S(1)} %get-tuple-element.7), kind=kLoop, calls=%fused_computation.4 | loop fusion | flops 524288 | bytes 4194304 | tf_op jit(solution)/shard_map/stack | solution.py:67
  43.3 3.2 %reshape.492 = f32[8,128,512]{2,1,0:T(8,128)S(1)} reshape(f32[1,8,2,32768]{3,2,1,0:T(2,128)} %pad_maximum_fusion) | data formatting | bytes 4194304 | tf_op jit(solution)/shard_map/reshape | solution.py:67
  46.6 3.2 %fusion.33 = f32[8,512,256]{1,2,0:T(8,128)S(1)} fusion(f32[8,128,512]{2,1,0:T(8,128)S(1)} %reshape.492, f32[128,64]{1,0:T(8,128)} %get-tuple-element.16, f32[128,64]{1,0:T(8,128)} %get-tuple-element.15, f32[128,64]{1,0:T(8,128)} %fusion.54), kind=kOutput, calls=%fused_computation.52 | convolution fusion | flops 805404672 | bytes 6389760 | tf_op jit(solution)/shard_map/uv,pvk->puk/dot_general | solution.py:68
  49.8 0.7 multiply_subtract_fusion
  50.5 2.1 %fusion.56 = f32[8]{0:T(128)S(1)} fusion(f32[1,8,32768]{2,0,1:T(1,128)} %get-tuple-element.10, f32[1,8,32768]{2,0,1:T(1,128)S(1)} %get-tuple-element.9, f32[1]{0:T(128)} %slice.60, f32[1]{0:T(128)} %slice.58), kind=kLoop, calls=%fused_computation.115 | loop fusion | flops 24 | bytes 104 | tf_op jit(solution)/shard_map/slice | solution.py:75
  52.5 2.0 %fusion.10 = f32[1,8,64,128]{3,2,1,0:T(8,128)S(1)} fusion(f32[8,1,128,512]{3,2,1,0:T(8,128)S(1)} %get-tuple-element.6, f32[8,1,128,512]{3,2,1,0:T(8,128)S(1)} %get-tuple-element.5, f32[64,1,512]{2,0,1:T(8,128)S(1)} %get-tuple-element.17, f32[64,1,512]{2,0,1:T(8,128)S(1)} %copy-done.1), kind=kOutput, calls=%fused_computation.9 | convolution fusion | flops 403832832 | bytes 4718592 | tf_op jit(solution)/shard_map/tck,pcuk->ptu/dot_general | solution.py:73
  55.7 0.6 constant_dynamic-update-slice_fusion.14
  65.3 5.4 %all-to-all-start = ((f32[16,1,1,8192]{3,2,1,0:T(1,128)}), f32[16,1,1,8192]{3,2,1,0:T(1,128)S(1)}, u32[]{:S(2)}, u32[]{:S(2)}) async-start(f32[16,1,1,8192]{3,2,1,0:T(1,128)} %constant_dynamic-update-slice_fusion), calls=%async_computation | async-start | bytes 1048576 | tf_op jit(solution)/shard_map/all_to_all | solution.py:128
  72.1 13.0 %all-to-all-done = f32[16,1,1,8192]{3,2,1,0:T(1,128)S(1)} async-done(((f32[16,1,1,8192]{3,2,1,0:T(1,128)}), f32[16,1,1,8192]{3,2,1,0:T(1,128)S(1)}, u32[]{:S(2)}, u32[]{:S(2)}) %all-to-all-start) | async-done | bytes 524320 | tf_op jit(solution)/shard_map/all_to_all | solution.py:128
  85.0 1.2 %fusion.20 = f32[1,16,8192]{2,1,0:T(8,128)} fusion(f32[16,1,1,8192]{3,2,1,0:T(1,128)S(1)} %all-to-all-done, f32[16]{0:T(128)S(1)} %fusion.57, pred[16]{0:T(512)(128)(4,1)S(1)} %iota_compare_fusion.1, s32[]{:T(128)S(6)} %select_n.86, f32[8,8192]{1,0:T(8,128)S(1)} %broadcast_in_dim.49, f32[8,8192]{1,0:T(8,128)S(1)} %fusion.24), kind=kLoop, calls=%fused_computation.28 | loop fusion | flops 786432 | bytes 1572948 | tf_op jit(solution)/shard_map/mul | solution.py:132
  (38 shorter events, 12.9 us)
Async XLA Ops:
  0.0 8.3 %collective-permute-start = (bf16[1,2,32768]{2,1,0:T(2,128)(2,1)}, bf16[1,2,32768]{2,1,0:T(2,128)(2,1)S(1)}, u32[]{:S(2)}, u32[]{:S(2)}) collective-permute-start(bf16[1,2,32768]{2,1,0:T(2,128)(2,1)} %param.3), channel_id=1, source_target_pairs={{0,15},{1,0},{2,1},{3,2},{4,3},{5,4},{6,5},{7,6},{8,7},{9,8},{10,9... | collective-permute-start | bytes 393224 | tf_op jit(solution)/shard_map/ppermute | solution.py:13
  5.4 18.3 %collective-permute-start.3 = (bf16[1,2,32768]{2,1,0:T(2,128)(2,1)}, bf16[1,2,32768]{2,1,0:T(2,128)(2,1)S(1)}, u32[]{:S(2)}, u32[]{:S(2)}) collective-permute-start(bf16[1,2,32768]{2,1,0:T(2,128)(2,1)} %param.3), channel_id=1, source_target_pairs={{0,8},{1,9},{2,10},{3,11},{4,12},{5,13},{6,14},{7,15},{8,0},{9,1},... | collective-permute-start | bytes 393224 | tf_op jit(solution)/shard_map/ppermute | solution.py:13
  9.6 8.0 %collective-permute-start.1 = (bf16[2,2,32768]{2,1,0:T(2,128)(2,1)S(1)}, bf16[2,2,32768]{2,1,0:T(2,128)(2,1)S(1)}, u32[]{:S(2)}, u32[]{:S(2)}) collective-permute-start(bf16[2,2,32768]{2,1,0:T(2,128)(2,1)S(1)} %pad_maximum_fusion.2), channel_id=1, source_target_pairs={{0,14},{1,15},{2,0},{3,1},{4,2},{5,3},{6,4},{7,5},{8,6},{9,7},{10,... | collective-permute-start | bytes 786440 | tf_op jit(solution)/shard_map/ppermute | solution.py:13
  19.2 13.9 %collective-permute-start.2 = (bf16[4,2,32768]{2,1,0:T(2,128)(2,1)S(1)}, bf16[4,2,32768]{2,1,0:T(2,128)(2,1)S(1)}, u32[]{:S(2)}, u32[]{:S(2)}) collective-permute-start(bf16[4,2,32768]{2,1,0:T(2,128)(2,1)S(1)} %pad_maximum_fusion.1), channel_id=1, source_target_pairs={{0,12},{1,13},{2,14},{3,15},{4,0},{5,1},{6,2},{7,3},{8,4},{9,5},{1... | collective-permute-start | bytes 1572872 | tf_op jit(solution)/shard_map/ppermute | solution.py:13
  46.5 3.2 %copy-start = (f32[128,512]{1,0:T(8,128)S(1)}, f32[128,512]{1,0:T(8,128)}, u32[]{:S(2)}) copy-start(f32[128,512]{1,0:T(8,128)} %get-tuple-element.14) | copy-start | bytes 786436
  49.8 2.8 %copy-start.1 = (f32[64,1,512]{2,0,1:T(8,128)S(1)}, f32[64,1,512]{2,0,1:T(8,128)}, u32[]{:S(2)}) copy-start(f32[64,1,512]{2,0,1:T(8,128)} %get-tuple-element.18) | copy-start | bytes 393220
  54.6 16.2 %copy-start.2 = (s32[16]{0:T(128)S(1)}, s32[16]{0:T(128)}, u32[]{:S(2)}) copy-start(s32[16]{0:T(128)} %param.5) | copy-start | bytes 196
  54.6 17.5 %copy-start.3 = (s32[1,16]{1,0:T(1,128)S(1)}, s32[1,16]{1,0:T(1,128)}, u32[]{:S(2)}) copy-start(s32[1,16]{1,0:T(1,128)} %param.4) | copy-start | bytes 196
  65.3 19.7 %all-to-all-start = ((f32[16,1,1,8192]{3,2,1,0:T(1,128)}), f32[16,1,1,8192]{3,2,1,0:T(1,128)S(1)}, u32[]{:S(2)}, u32[]{:S(2)}) async-start(f32[16,1,1,8192]{3,2,1,0:T(1,128)} %constant_dynamic-update-slice_fusion), calls=%async_computation | async-start | bytes 1048576 | tf_op jit(solution)/shard_map/all_to_all | solution.py:128
